TPU v7x, 32 devices: a whole 2x2x4 slice. The times are simulated.
32 devices in a mesh: ga: 8 (over y, x, core), ba: 4 (over z).
Axes of the slice: x: 2, y: 2, z: 4, core: 2. Of those that a mesh axis runs over, the one named last changes fastest.
Arguments:
- psi: float32 [2, 16384, 2048], P(None, 'ga', 'ba'), may hold values from -0.1875 to 0.1875
- dpsi: float32 [2, 16384, 512], P(None, 'ga', 'ba'), may hold values from -6 to 6
- band_weight: float32 [2048], replicated, may hold values from 0.25 to 1
- panel_band: int32 [16], P('ba'), may hold values from 0 to 15, each once
- slab_offset: int32 [8], replicated, may hold values from 0 to 2047
Outputs:
- projected: float32 [2, 16384, 512], P(None, 'ga', 'ba')
Inputs may be any that keep to these rules, and one draw needn't show every extreme that they name: panel_band is a permutation of the panel numbers.
All inputs are finite; a program needn't handle non-finite values.
Results may differ from a plain program's by a relative error of at most 0.00012.
Values sent between devices are 32-bit elements; how exact they have to be, the bound alone decides.
A program may use at most 128 MiB of HBM per device.

v0:
```python
import jax
import jax.numpy as jnp
from jax import lax
from jax.sharding import PartitionSpec as P

PANEL = 128


def tdot(left, right):
    return lax.dot_general(
        left,
        right,
        (((0,), (0,)), ((), ())),
        precision=lax.Precision.HIGHEST,
        preferred_element_type=jnp.float32,
    )


def mdot(left, right):
    return jnp.dot(left, right, precision=lax.Precision.HIGHEST, preferred_element_type=jnp.float32)


def margin_of(waves, columns):
    over_re = tdot(waves[0], columns[0]) + tdot(waves[1], columns[1])
    over_im = tdot(waves[0], columns[1]) - tdot(waves[1], columns[0])
    return jnp.stack([over_re, over_im])


def correct_with(waves, weighted):
    corr_re = mdot(waves[0], weighted[0]) - mdot(waves[1], weighted[1])
    corr_im = mdot(waves[0], weighted[1]) + mdot(waves[1], weighted[0])
    return jnp.stack([corr_re, corr_im])


def weights_for(band_weight, panels):
    table = band_weight.reshape(-1, PANEL)
    onehot = (panels[:, None] == jnp.arange(table.shape[0], dtype=jnp.int32)[None, :]).astype(
        jnp.float32
    )
    return mdot(onehot, table).reshape(-1)


def per_device(psi, dpsi, band_weight, panel_band, slab_offset):
    offset = slab_offset[lax.axis_index("ga")]
    aligned = jnp.roll(dpsi, -offset, axis=1)
    local_weight = weights_for(band_weight, panel_band)
    blocks = margin_of(psi, lax.all_gather(aligned, "ba", axis=2, tiled=True))
    margin = lax.psum(blocks, "ga")
    weighted = margin * local_weight[None, :, None]
    correction = correct_with(psi, weighted)
    share = lax.psum_scatter(correction, "ba", scatter_dimension=2, tiled=True)
    result = aligned - share
    return jnp.roll(result, offset, axis=1)


def solution(mesh):
    in_specs = (P(None, "ga", "ba"), P(None, "ga", "ba"), P(), P("ba"), P())
    out_specs = P(None, "ga", "ba")
    return jax.shard_map(
        per_device, mesh=mesh, in_specs=in_specs, out_specs=out_specs, check_vma=False
    )
```

profile of v0, /device:TPU:0, one launch (start us, length us, event | category | flops | bytes accessed | tf_op | source)
XLA Modules:
  0.0 466.1 jit_solution(3996148815091841346)
XLA Ops:
  6.5 1.3 dynamic_slice.6
  9.1 1.9 copy.6
  11.0 2.5 fusion.29
  13.5 0.0 all-gather.2.cloned.1.call-update
  13.5 0.0 all-reduce.2.cloned.1.call-start
  13.6 152.4 %all-gather.2.cloned.1.call-done = f32[2,2048,512]{1,2,0:T(8,128)} async-done(((f32[2,2048,128]{1,2,0:T(8,128)}), f32[2,2048,512]{1,2,0:T(8,128)}) %all-gather.2.cloned.1.call-update) | async-done | bytes 8388624 | tf_op jit(solution)/shard_map/all_gather | solution.py:47
  166.0 9.4 %fusion.4 = f32[512,512]{1,0:T(8,128)S(1)} fusion(f32[2,2048,512]{1,2,0:T(8,128)} %all-gather.2.cloned.1.call-done, f32[2,2048,512]{2,1,0:T(8,128)} %param.7), kind=kOutput, calls=%fused_computation.11 | convolution fusion | flops 6442450944 | bytes 9437184 | tf_op jit(solution)/shard_map/dot_general | solution.py:10
  175.5 0.0 slice-start.1
  175.5 0.0 slice-start.5
  175.5 21.7 %fusion.6 = f32[512,512]{1,0:T(8,128)S(1)} fusion(f32[2,2048,512]{1,2,0:T(8,128)} %all-gather.2.cloned.1.call-done, f32[2,2048,512]{2,1,0:T(8,128)} %param.7), kind=kOutput, calls=%fused_computation.13 | convolution fusion | flops 6442450944 | bytes 9437184 | tf_op jit(solution)/shard_map/dot_general | solution.py:10
  197.3 6.8 %fusion.39 = f32[1,512,512]{1,2,0:T(8,128)S(1)} fusion(f32[512,512]{1,0:T(8,128)S(1)} %fusion.4, f32[2,2048,512]{2,1,0:T(8,128)S(1)} %bitcast.77, f32[2,2048,512]{1,2,0:T(8,128)S(1)} %bitcast.81), kind=kOutput, calls=%fused_computation.39 | convolution fusion | flops 6442713088 | bytes 10485760 | tf_op jit(solution)/shard_map/dot_general | solution.py:10
  204.1 6.8 %fusion.33 = f32[1,512,512]{1,2,0:T(8,128)S(1)} fusion(f32[512,512]{1,0:T(8,128)S(1)} %fusion.6, f32[2,2048,512]{2,1,0:T(8,128)S(1)} %bitcast.77, f32[2,2048,512]{1,2,0:T(8,128)S(1)} %bitcast.81), kind=kOutput, calls=%fused_computation.37 | convolution fusion | flops 6442713088 | bytes 10485760 | tf_op jit(solution)/shard_map/dot_general | solution.py:10
  211.0 0.0 copy-start.2
  211.0 1.5 pad_maximum_fusion.1
  212.5 0.0 all-reduce.2.cloned.1.call-update
  212.5 0.0 reduce-scatter.2.cloned.1.call-start
  212.5 0.0 copy-done
  212.6 0.0 copy-done.2
  212.6 0.2 convolution_bitcast_fusion
  212.8 59.8 %all-reduce.2.cloned.1.call-done = f32[2,512,512]{1,2,0:T(8,128)} async-done(((f32[2,512,512]{1,2,0:T(8,128)}), f32[2,512,512]{1,2,0:T(8,128)}) %all-reduce.2.cloned.1.call-update) | async-done | bytes 2097168 | tf_op jit(solution)/shard_map/psum | solution.py:48
  272.6 2.0 broadcast_multiply_fusion
  274.6 0.0 slice-start.3
  274.6 9.4 %fusion = f32[512,2048]{1,0:T(8,128)S(1)} fusion(f32[2,2048,512]{2,1,0:T(8,128)} %param.7, f32[2,512,512]{1,2,0:T(8,128)S(1)} %broadcast_multiply_fusion), kind=kOutput, calls=%fused_computation.7 | convolution fusion | flops 6442450944 | bytes 9437184 | tf_op jit(solution)/shard_map/dot_general | solution.py:20
  284.1 7.2 %fusion.2 = f32[512,2048]{1,0:T(8,128)S(1)} fusion(f32[2,2048,512]{2,1,0:T(8,128)S(1)} %bitcast.79, f32[2,512,512]{1,2,0:T(8,128)S(1)} %broadcast_multiply_fusion), kind=kOutput, calls=%fused_computation.9 | convolution fusion | flops 6442450944 | bytes 9437184 | tf_op jit(solution)/shard_map/dot_general | solution.py:20
  291.3 7.4 %add_bitcast_fusion = f32[1,2048,512]{1,2,0:T(8,128)S(1)} fusion(f32[512,2048]{1,0:T(8,128)S(1)} %fusion, f32[2,2048,512]{2,1,0:T(8,128)S(1)} %bitcast.79, f32[2,512,512]{1,2,0:T(8,128)S(1)} %broadcast_multiply_fusion), kind=kOutput, calls=%fused_computation.23 | convolution fusion | flops 6443499520 | bytes 13631488 | tf_op jit(solution)/shard_map/dot_general | solution.py:20
  298.7 7.2 %subtract_bitcast_fusion = f32[1,2048,512]{1,2,0:T(8,128)S(1)} fusion(f32[512,2048]{1,0:T(8,128)S(1)} %fusion.2, f32[2,2048,512]{2,1,0:T(8,128)S(1)} %bitcast.79, f32[2,512,512]{1,2,0:T(8,128)S(1)} %broadcast_multiply_fusion), kind=kOutput, calls=%fused_computation.24 | convolution fusion | flops 6443499520 | bytes 13631488 | tf_op jit(solution)/shard_map/dot_general | solution.py:20
  306.0 3.8 pad_maximum_fusion
  309.8 0.0 reduce-scatter.2.cloned.1.call-update
  311.1 142.6 %reduce-scatter.2.cloned.1.call-done = f32[2,2048,128]{1,2,0:T(8,128)} async-done(((f32[2,2048,512]{1,2,0:T(8,128)}), f32[2,2048,128]{1,2,0:T(8,128)}) %reduce-scatter.2.cloned.1.call-update) | async-done | bytes 2097168 | tf_op jit(solution)/shard_map/reduce_scatter | solution.py:51
  453.7 2.8 fusion.44
  456.4 1.2 fusion.28
  457.6 1.8 copy.8
  (16 shorter events, 0.0 us)
Async XLA Ops:
  6.5 206.0 %copy-start = (f32[2048]{0:T(1024)S(1)}, f32[2048]{0:T(1024)}, u32[]{:S(2)}) copy-start(f32[2048]{0:T(1024)} %param.9) | copy-start | bytes 24580
  6.5 159.5 %all-gather.2.cloned.1.call-start = ((), (), s32[]{:S(2)}) async-start(), calls=%async_computation.1 | async-start | bytes 10485760 | tf_op jit(solution)/shard_map/all_gather | solution.py:47
  13.5 259.0 %all-reduce.2.cloned.1.call-start = ((), (), s32[]{:S(2)}) async-start(), calls=%async_computation.2 | async-start | bytes 4194304 | tf_op jit(solution)/shard_map/psum | solution.py:48
  166.0 31.2 %slice-start = ((s8[8388608]{0:T(1024)(128)(4,1)}), s8[4194304]{0:T(1024)(128)(4,1)S(1)}, s32[]{:S(2)}) async-start(s8[8388608]{0:T(1024)(128)(4,1)} %bitcast.76), calls=%async_computation.4 | async-start | bytes 8388608
  166.0 31.2 %slice-start.4 = ((s8[8388608]{0:T(1024)(128)(4,1)}), s8[4194304]{0:T(1024)(128)(4,1)S(1)}, s32[]{:S(2)}) async-start(s8[8388608]{0:T(1024)(128)(4,1)} %bitcast.80), calls=%async_computation.8 | async-start | bytes 8388608
  175.5 21.7 %slice-start.1 = ((s8[8388608]{0:T(1024)(128)(4,1)}), s8[4194304]{0:T(1024)(128)(4,1)S(1)}, s32[]{:S(2)}) async-start(s8[8388608]{0:T(1024)(128)(4,1)} %bitcast.76), calls=%async_computation.5 | async-start | bytes 8388608
  175.5 21.7 %slice-start.5 = ((s8[8388608]{0:T(1024)(128)(4,1)}), s8[4194304]{0:T(1024)(128)(4,1)S(1)}, s32[]{:S(2)}) async-start(s8[8388608]{0:T(1024)(128)(4,1)} %bitcast.80), calls=%async_computation.9 | async-start | bytes 8388608
  211.0 1.6 copy-start.2
  212.5 241.2 %reduce-scatter.2.cloned.1.call-start = ((), (), s32[]{:S(2)}) async-start(), calls=%async_computation.3 | async-start | bytes 10485760 | tf_op jit(solution)/shard_map/reduce_scatter | solution.py:51
  272.6 11.5 %slice-start.2 = ((s8[8388608]{0:T(1024)(128)(4,1)}), s8[4194304]{0:T(1024)(128)(4,1)S(1)}, s32[]{:S(2)}) async-start(s8[8388608]{0:T(1024)(128)(4,1)} %bitcast.78), calls=%async_computation.6 | async-start | bytes 8388608
  274.6 9.5 %slice-start.3 = ((s8[8388608]{0:T(1024)(128)(4,1)}), s8[4194304]{0:T(1024)(128)(4,1)S(1)}, s32[]{:S(2)}) async-start(s8[8388608]{0:T(1024)(128)(4,1)} %bitcast.78), calls=%async_computation.7 | async-start | bytes 8388608
  453.7 5.7 %copy-start.1 = (f32[2048]{0:T(1024)S(1)}, f32[2048]{0:T(1024)}, u32[]{:S(2)}) copy-start(f32[2048]{0:T(1024)} %param.9) | copy-start | bytes 24580
Sparse Core Ops, SparseCore 0:
  13.7 152.3 all-gather.1
  212.6 59.9 all-reduce.1
  309.9 143.6 reduce-scatter.1
where the time goes:
time: 472 us; the launch traced here: 466 us
  waiting for transfers between devices  355 us (75%)
  matrix products  76.3 us (16%)
  between operations  16 us (3%)
  other arithmetic  13.7 us (3%)
  local copies, waits for them, and re-layouts  5.08 us (1%)
    all_gather x1, waiting for transfers between devices, per_device(): blocks = margin_of(psi, lax.all_gather(aligned, 'ba', axis=2, tiled=True))  152 us
    reduce_scatter x1, waiting for transfers between devices, per_device(): share = lax.psum_scatter(correction, 'ba', scatter_dimension=2, tiled=True)  143 us
    psum x1, waiting for transfers between devices, per_device(): margin = lax.psum(blocks, 'ga')  59.8 us
    dot_general x4, matrix products, tdot(): lax.dot_general(left, right, (((0,), (0,)), ((), ())), precision=lax.Prec...  44.8 us
    dot_general x5, matrix products, mdot(): jnp.dot(left, right, precision=lax.Precision.HIGHEST, preferred_element_t...  31.5 us
  transfers between devices with their start and end apart: 3, of which 3 were waited for; matrix products, arithmetic and copies ran while one was open for 0% of the time, Pallas kernels for 0%

commit v1 on v0

--- a/solution.py
+++ b/solution.py
@@ -45,7 +45,9 @@
     aligned = jnp.roll(dpsi, -offset, axis=1)
     local_weight = weights_for(band_weight, panel_band)
     blocks = margin_of(psi, lax.all_gather(aligned, "ba", axis=2, tiled=True))
-    margin = lax.psum(blocks, "ga")
+    margin = blocks
+    for hop in (1, 2, 4):
+        margin = margin + lax.ppermute(margin, "ga", [(dev, dev ^ hop) for dev in range(8)])
     weighted = margin * local_weight[None, :, None]
     correction = correct_with(psi, weighted)
     share = lax.psum_scatter(correction, "ba", scatter_dimension=2, tiled=True)

time: 472 us -> 496 us (1.051)
  waiting for transfers between devices: 355 us -> 390 us
  matrix products: 76.3 us -> 63.1 us
    ppermute x0 -> x3, waiting for transfers between devices: none -> 95.5 us  [per_device(): lax.ppermute(margin, 'ga', [(dev, dev ^ hop) for dev in range(8)])]
    psum x1 -> x0, waiting for transfers between devices: 59.8 us -> none  [per_device(): margin = lax.psum(blocks, 'ga')]
    dot_general x4, matrix products: 44.8 us -> 33.5 us  [tdot(): lax.dot_general(left, right, (((0,), (0,)), ((), ())), precision=lax.Prec...]
  transfers between devices with their start and end apart: 3 -> 5, of which waited for: 3 -> 5; matrix products, arithmetic and copies ran while one was open for 0% -> 0% of each run, Pallas kernels for 0% -> 0%
where the time goes in v1:
time: 496 us; the launch traced here: 490 us
  waiting for transfers between devices  390 us (79%)
  matrix products  63.1 us (13%)
  between operations  16.3 us (3%)
  other arithmetic  12.3 us (2%)
  local copies, waits for them, and re-layouts  5.04 us (1%)
    all_gather x1, waiting for transfers between devices, per_device(): blocks = margin_of(psi, lax.all_gather(aligned, 'ba', axis=2, tiled=True))  152 us
    reduce_scatter x1, waiting for transfers between devices, per_device(): share = lax.psum_scatter(correction, 'ba', scatter_dimension=2, tiled=True)  142 us
    ppermute x3, waiting for transfers between devices, per_device(): lax.ppermute(margin, 'ga', [(dev, dev ^ hop) for dev in range(8)])  95.5 us
    dot_general x4, matrix products, tdot(): lax.dot_general(left, right, (((0,), (0,)), ((), ())), precision=lax.Prec...  33.5 us
    dot_general x5, matrix products, mdot(): jnp.dot(left, right, precision=lax.Precision.HIGHEST, preferred_element_t...  29.6 us
  transfers between devices with their start and end apart: 5, of which 5 were waited for; matrix products, arithmetic and copies ran while one was open for 0% of the time, Pallas kernels for 0%

profile of v1, /device:TPU:0, one launch (start us, length us, event | category | flops | bytes accessed | tf_op | source)
XLA Modules:
  0.0 489.6 jit_solution(3209374711186903793)
XLA Ops:
  6.5 1.3 dynamic_slice.6
  9.1 1.9 copy.6
  11.0 2.5 fusion.29
  13.5 0.0 all-gather.2.cloned.1.call-update
  13.5 0.0 reduce-scatter.2.cloned.1.call-start
  13.6 152.4 %all-gather.2.cloned.1.call-done = f32[2,2048,512]{1,2,0:T(8,128)} async-done(((f32[2,2048,128]{1,2,0:T(8,128)}), f32[2,2048,512]{1,2,0:T(8,128)}) %all-gather.2.cloned.1.call-update) | async-done | bytes 8388624 | tf_op jit(solution)/shard_map/all_gather | solution.py:47
  166.0 9.5 %fusion.4 = f32[512,512]{1,0:T(8,128)S(1)} fusion(f32[2,2048,512]{1,2,0:T(8,128)} %all-gather.2.cloned.1.call-done, f32[2,2048,512]{2,1,0:T(8,128)} %param.7), kind=kOutput, calls=%fused_computation.11 | convolution fusion | flops 6442450944 | bytes 9437184 | tf_op jit(solution)/shard_map/dot_general | solution.py:10
  175.5 0.0 slice-start.1
  175.5 10.3 %fusion.6 = f32[512,512]{1,0:T(8,128)S(1)} fusion(f32[2,2048,512]{1,2,0:T(8,128)} %all-gather.2.cloned.1.call-done, f32[2,2048,512]{2,1,0:T(8,128)} %param.7), kind=kOutput, calls=%fused_computation.13 | convolution fusion | flops 6442450944 | bytes 9437184 | tf_op jit(solution)/shard_map/dot_general | solution.py:10
  185.9 6.8 %fusion.39 = f32[1,512,512]{1,2,0:T(8,128)S(1)} fusion(f32[512,512]{1,0:T(8,128)S(1)} %fusion.4, f32[2,2048,512]{2,1,0:T(8,128)S(1)} %bitcast.77, f32[2,2048,512]{1,2,0:T(8,128)S(1)} %bitcast.79), kind=kOutput, calls=%fused_computation.40 | convolution fusion | flops 6442713088 | bytes 10485760 | tf_op jit(solution)/shard_map/dot_general | solution.py:10
  192.8 6.8 %fusion.33 = f32[1,512,512]{1,2,0:T(8,128)S(1)} fusion(f32[512,512]{1,0:T(8,128)S(1)} %fusion.6, f32[2,2048,512]{2,1,0:T(8,128)S(1)} %bitcast.77, f32[2,2048,512]{1,2,0:T(8,128)S(1)} %bitcast.79), kind=kOutput, calls=%fused_computation.38 | convolution fusion | flops 6442713088 | bytes 10485760 | tf_op jit(solution)/shard_map/dot_general | solution.py:10
  199.6 0.2 pad_maximum_fusion.1
  199.8 0.1 collective-permute-start
  199.9 4.1 collective-permute-done
  204.0 0.7 fusion.44
  204.7 1.5 collective-permute-start.1
  206.3 46.2 %collective-permute-done.1 = f32[2,512,512]{1,2,0:T(8,128)S(1)} collective-permute-done((f32[2,512,512]{1,2,0:T(8,128)S(1)}, f32[2,512,512]{1,2,0:T(8,128)S(1)}, u32[]{:S(2)}, u32[]{:S(2)}) %collective-permute-start.1) | collective-permute-done | bytes 2097184 | tf_op jit(solution)/shard_map/ppermute | solution.py:50
  252.5 0.8 fusion.46
  253.2 1.5 collective-permute-start.2
  254.8 0.2 convolution_bitcast_fusion
  254.9 45.2 %collective-permute-done.2 = f32[2,512,512]{1,2,0:T(8,128)S(1)} collective-permute-done((f32[2,512,512]{1,2,0:T(8,128)S(1)}, f32[2,512,512]{1,2,0:T(8,128)S(1)}, u32[]{:S(2)}, u32[]{:S(2)}) %collective-permute-start.2) | collective-permute-done | bytes 2097184 | tf_op jit(solution)/shard_map/ppermute | solution.py:50
  300.1 0.5 add_multiply_fusion
  300.6 7.2 %fusion = f32[512,2048]{1,0:T(8,128)S(1)} fusion(f32[2,2048,512]{2,1,0:T(8,128)S(1)} %bitcast.77, f32[2,512,512]{1,2,0:T(8,128)S(1)} %add_multiply_fusion), kind=kOutput, calls=%fused_computation.7 | convolution fusion | flops 6442450944 | bytes 9437184 | tf_op jit(solution)/shard_map/dot_general | solution.py:20
  307.8 7.6 %fusion.2 = f32[512,2048]{1,0:T(8,128)S(1)} fusion(f32[2,2048,512]{2,1,0:T(8,128)S(1)} %bitcast.77, f32[2,512,512]{1,2,0:T(8,128)S(1)} %add_multiply_fusion), kind=kOutput, calls=%fused_computation.9 | convolution fusion | flops 6442450944 | bytes 9437184 | tf_op jit(solution)/shard_map/dot_general | solution.py:20
  315.4 7.2 %add_bitcast_fusion = f32[1,2048,512]{1,2,0:T(8,128)S(1)} fusion(f32[512,2048]{1,0:T(8,128)S(1)} %fusion, f32[2,2048,512]{2,1,0:T(8,128)S(1)} %bitcast.77, f32[2,512,512]{1,2,0:T(8,128)S(1)} %add_multiply_fusion), kind=kOutput, calls=%fused_computation.23 | convolution fusion | flops 6443499520 | bytes 13631488 | tf_op jit(solution)/shard_map/dot_general | solution.py:20
  322.6 7.4 %subtract_bitcast_fusion = f32[1,2048,512]{1,2,0:T(8,128)S(1)} fusion(f32[512,2048]{1,0:T(8,128)S(1)} %fusion.2, f32[2,2048,512]{2,1,0:T(8,128)S(1)} %bitcast.77, f32[2,512,512]{1,2,0:T(8,128)S(1)} %add_multiply_fusion), kind=kOutput, calls=%fused_computation.24 | convolution fusion | flops 6443499520 | bytes 13631488 | tf_op jit(solution)/shard_map/dot_general | solution.py:20
  330.1 3.8 pad_maximum_fusion
  333.9 0.0 reduce-scatter.2.cloned.1.call-update
  335.2 141.7 %reduce-scatter.2.cloned.1.call-done = f32[2,2048,128]{1,2,0:T(8,128)} async-done(((f32[2,2048,512]{1,2,0:T(8,128)}), f32[2,2048,128]{1,2,0:T(8,128)}) %reduce-scatter.2.cloned.1.call-update) | async-done | bytes 2097168 | tf_op jit(solution)/shard_map/reduce_scatter | solution.py:53
  476.9 2.8 fusion.45
  479.6 1.2 fusion.28
  480.8 1.8 copy.8
  (16 shorter events, 0.0 us)
Async XLA Ops:
  6.5 248.2 %copy-start = (f32[2048]{0:T(1024)S(1)}, f32[2048]{0:T(1024)}, u32[]{:S(2)}) copy-start(f32[2048]{0:T(1024)} %param.9) | copy-start | bytes 24580
  6.5 159.5 %all-gather.2.cloned.1.call-start = ((), (), s32[]{:S(2)}) async-start(), calls=%async_computation.1 | async-start | bytes 10485760 | tf_op jit(solution)/shard_map/all_gather | solution.py:47
  13.5 463.3 %reduce-scatter.2.cloned.1.call-start = ((), (), s32[]{:S(2)}) async-start(), calls=%async_computation.2 | async-start | bytes 10485760 | tf_op jit(solution)/shard_map/reduce_scatter | solution.py:53
  166.0 19.8 %slice-start = ((s8[8388608]{0:T(1024)(128)(4,1)}), s8[4194304]{0:T(1024)(128)(4,1)S(1)}, s32[]{:S(2)}) async-start(s8[8388608]{0:T(1024)(128)(4,1)} %bitcast.76), calls=%async_computation.3 | async-start | bytes 8388608
  166.0 19.8 %slice-start.2 = ((s8[8388608]{0:T(1024)(128)(4,1)}), s8[4194304]{0:T(1024)(128)(4,1)S(1)}, s32[]{:S(2)}) async-start(s8[8388608]{0:T(1024)(128)(4,1)} %bitcast.78), calls=%async_computation.5 | async-start | bytes 8388608
  175.5 10.4 %slice-start.1 = ((s8[8388608]{0:T(1024)(128)(4,1)}), s8[4194304]{0:T(1024)(128)(4,1)S(1)}, s32[]{:S(2)}) async-start(s8[8388608]{0:T(1024)(128)(4,1)} %bitcast.76), calls=%async_computation.4 | async-start | bytes 8388608
  175.5 10.4 %slice-start.3 = ((s8[8388608]{0:T(1024)(128)(4,1)}), s8[4194304]{0:T(1024)(128)(4,1)S(1)}, s32[]{:S(2)}) async-start(s8[8388608]{0:T(1024)(128)(4,1)} %bitcast.78), calls=%async_computation.6 | async-start | bytes 8388608
  199.8 4.2 collective-permute-start
  204.7 50.0 %copy-start.2 = (s32[4]{0:T(128)S(1)}, s32[4]{0:T(128)}, u32[]{:S(2)}) copy-start(s32[4]{0:T(128)} %param.10) | copy-start | bytes 52
  204.7 47.7 %collective-permute-start.1 = (f32[2,512,512]{1,2,0:T(8,128)S(1)}, f32[2,512,512]{1,2,0:T(8,128)S(1)}, u32[]{:S(2)}, u32[]{:S(2)}) collective-permute-start(f32[2,512,512]{1,2,0:T(8,128)S(1)} %fusion.44), channel_id=1, source_target_pairs={{0,8},{4,12},{8,0},{12,4},{16,24},{20,28},{24,16},{28,20},{1,9},{5... | collective-permute-start | bytes 6291464 | tf_op jit(solution)/shard_map/ppermute | solution.py:50
  253.2 46.9 %collective-permute-start.2 = (f32[2,512,512]{1,2,0:T(8,128)S(1)}, f32[2,512,512]{1,2,0:T(8,128)S(1)}, u32[]{:S(2)}, u32[]{:S(2)}) collective-permute-start(f32[2,512,512]{1,2,0:T(8,128)S(1)} %fusion.46), channel_id=1, source_target_pairs={{0,16},{4,20},{8,24},{12,28},{16,0},{20,4},{24,8},{28,12},{1,17},{... | collective-permute-start | bytes 6291464 | tf_op jit(solution)/shard_map/ppermute | solution.py:50
  476.9 5.7 %copy-start.1 = (f32[2048]{0:T(1024)S(1)}, f32[2048]{0:T(1024)}, u32[]{:S(2)}) copy-start(f32[2048]{0:T(1024)} %param.9) | copy-start | bytes 24580
Sparse Core Ops, SparseCore 0:
  13.7 152.3 all-gather.1
  334.0 142.7 reduce-scatter.1
